TPU v7x, 32 devices: a whole 2x2x4 slice. The times are simulated.
32 devices in a mesh: dp: 4 (over y, core), expert: 4 (over z), tensor: 2 (over x).
Axes of the slice: x: 2, y: 2, z: 4, core: 2. Of those that a mesh axis runs over, the one named last changes fastest.
Arguments:
- router_input: bfloat16 [1024, 2048], P(('dp', 'expert'), 'tensor'), may hold values from -6 to 6
- router_weight: bfloat16 [2048, 8], replicated, may hold values from -0.125 to 0.125
- expert_ids: int32 [1024, 2], P(('dp', 'expert', 'tensor')), may hold values from 0 to 7, all different within a row; in each aligned block of 32 rows (0 to 31, 32 to 63, ...) at most 9 rows name the same one
- down_weight: bfloat16 [61440, 2048], P(('expert', 'tensor')), may hold values from -0.0625 to 0.0625
- hidden: bfloat16 [4, 72, 61440], P('dp', None, ('expert', 'tensor')), may hold values from -6 to 6
- grad_output: bfloat16 [1024, 2048], P(('dp', 'expert', 'tensor')), may hold values from -4 to 4
Outputs:
- weight_grad: bfloat16 [61440, 2048], P(('expert', 'tensor', 'dp'))
- hidden_grad: bfloat16 [4, 72, 61440], P('dp', None, ('expert', 'tensor'))
- router_grad: float32 [2048, 8], replicated
- input_grad: bfloat16 [1024, 2048], P(('dp', 'expert', 'tensor'))
Inputs may be any that keep to these rules, and one draw needn't show every extreme that they name: `expert_ids`: each row names 2 different experts. Within the 32 rows of one device no expert is named more than 9 times, and some device's rows name some expert exactly 9 times.
All inputs are finite; a program needn't handle non-finite values.
Results may differ from a plain program's by a relative error of at most 0.018.
Values may be sent and summed in bfloat16 or wider, within the bound.
No kernel may reach another device: no remote copies, remote signals or barrier semaphores. Data moves between devices by JAX's collectives and lax.ppermute only.
A program may use at most 192 MiB of HBM per device.

v0:
```python
import jax
import jax.numpy as jnp
from jax import lax
from jax.sharding import PartitionSpec as P


def per_device(router_input, router_weight, expert_ids, down_weight, hidden, grad_output):
    token_rows = grad_output.shape[0]
    model_width = grad_output.shape[1]
    expert_count = router_weight.shape[1]
    choose_count = expert_ids.shape[1]
    expert_ranks = lax.axis_size("expert")
    tensor_ranks = lax.axis_size("tensor")
    sources = expert_ranks * tensor_ranks
    spread = sources // expert_count
    capacity = hidden.shape[1] // sources
    full_input = lax.all_to_all(router_input, "tensor", split_axis=0, concat_axis=1, tiled=True)
    logits = jnp.dot(full_input, router_weight, preferred_element_type=jnp.float32)
    labels = jnp.arange(expert_count, dtype=jnp.int32)
    onehot_int = (expert_ids[:, :, None] == labels).astype(jnp.int32)
    onehot = onehot_int.astype(jnp.float32)
    picked = jnp.sum(onehot * logits[:, None, :], axis=2)
    first_gate = jax.nn.sigmoid(picked[:, 0] - picked[:, 1])
    second_gate = jax.nn.sigmoid(picked[:, 1] - picked[:, 0])
    gate_values = jnp.stack([first_gate, second_gate], axis=1)
    gate_low = gate_values.astype(jnp.bfloat16)
    flat_hits = onehot_int.reshape(token_rows * choose_count, expert_count)
    before = jnp.cumsum(flat_hits, axis=0) - flat_hits
    slot_pos = jnp.sum(before * flat_hits, axis=1).reshape(token_rows, choose_count)
    slot_ids = jnp.arange(capacity, dtype=jnp.int32)
    dispatch_table = onehot[:, :, :, None] * (slot_pos[:, :, None, None] == slot_ids).astype(
        jnp.float32
    )
    slot_table = jnp.sum(dispatch_table, axis=1).astype(jnp.bfloat16)
    packed_grad = jnp.einsum(
        "rec,rd->ecd", slot_table, grad_output, preferred_element_type=jnp.float32
    ).astype(jnp.bfloat16)
    packed_gate = jnp.einsum("rkec,rk->ec", dispatch_table, gate_low.astype(jnp.float32)).astype(
        jnp.bfloat16
    )
    send_grad = jnp.repeat(packed_grad, spread, axis=0)
    send_gate = jnp.repeat(packed_gate, spread, axis=0)
    recv_grad, recv_gate = (
        lax.all_to_all(send_grad, ("expert", "tensor"), split_axis=0, concat_axis=0, tiled=True),
        lax.all_to_all(send_gate, ("expert", "tensor"), split_axis=0, concat_axis=0, tiled=True),
    )
    recv_grad = recv_grad.reshape(sources * capacity, model_width)
    recv_gate = recv_gate.reshape(sources * capacity).astype(jnp.float32)
    hidden_rows = hidden[0]
    gated_grad = (recv_gate[:, None] * recv_grad.astype(jnp.float32)).astype(jnp.bfloat16)
    expert_image = lax.dot_general(
        recv_grad, down_weight, (((1,), (1,)), ((), ())), preferred_element_type=jnp.float32
    )
    hidden_part = (recv_gate[:, None] * expert_image).astype(jnp.bfloat16)
    gate_partial = jnp.sum(hidden_rows.astype(jnp.float32) * expert_image, axis=1).reshape(
        sources, capacity
    )
    returned = lax.all_to_all(
        gate_partial, ("expert", "tensor"), split_axis=0, concat_axis=0, tiled=True
    )
    expert_sums = jnp.sum(returned.reshape(expert_count, spread, capacity), axis=1)
    gate_grad = jnp.einsum("rkec,ec->rk", dispatch_table, expert_sums)
    mixed_term = jnp.sum(gate_values * gate_grad, axis=1, keepdims=True)
    logit_part = gate_values * (gate_grad - mixed_term)
    logit_grad = jnp.sum(onehot * logit_part[:, :, None], axis=1)
    input_grad = jnp.dot(
        logit_grad, router_weight.astype(jnp.float32).T, precision=lax.Precision.HIGHEST
    ).astype(jnp.bfloat16)
    router_local = jnp.dot(
        full_input.astype(jnp.float32).T, logit_grad, precision=lax.Precision.HIGHEST
    )
    router_grad = lax.psum(router_local, ("dp", "expert", "tensor"))
    weight_sum = lax.psum_scatter(
        lax.dot_general(
            hidden_rows, gated_grad, (((0,), (0,)), ((), ())), preferred_element_type=jnp.float32
        ).astype(jnp.bfloat16),
        "dp",
        scatter_dimension=0,
        tiled=True,
    )
    return (weight_sum, hidden_part[None], router_grad, input_grad)


def solution(mesh):
    return jax.shard_map(
        per_device,
        mesh=mesh,
        in_specs=(
            P(("dp", "expert"), "tensor"),
            P(),
            P(("dp", "expert", "tensor"), None),
            P(("expert", "tensor"), None),
            P("dp", None, ("expert", "tensor")),
            P(("dp", "expert", "tensor"), None),
        ),
        out_specs=(
            P(("expert", "tensor", "dp"), None),
            P("dp", None, ("expert", "tensor")),
            P(),
            P(("dp", "expert", "tensor"), None),
        ),
        check_vma=False,
    )
```

profile of v0, /device:TPU:0, one launch (start us, length us, event | category | flops | bytes accessed | tf_op | source)
XLA Modules:
  0.0 359.2 jit_solution(10456292851233868904)
XLA Ops:
  8.0 4.4 %all-to-all-start = ((bf16[2,32,1024]{2,1,0:T(8,128)(2,1)}), bf16[2,32,1024]{2,1,0:T(8,128)(2,1)S(1)}, u32[]{:S(2)}, u32[]{:S(2)}) async-start(bf16[2,32,1024]{2,1,0:T(8,128)(2,1)} %bitcast.52), calls=%async_computation | async-start | bytes 262144 | tf_op jit(solution)/shard_map/all_to_all | solution.py:17
  12.4 0.8 copy.28
  13.2 0.7 convert_convert_fusion
  14.5 2.4 all-to-all-done
  17.0 0.9 fusion.15
  17.9 0.7 multiply_reduce_fusion.3
  18.9 0.6 copy.31
  19.5 5.4 %all-to-all-start.1 = ((bf16[8,1,9]{2,1,0:T(2,128)(2,1)}), bf16[8,1,9]{2,1,0:T(2,128)(2,1)S(1)}, u32[]{:S(2)}, u32[]{:S(2)}) async-start(bf16[8,1,9]{2,1,0:T(2,128)(2,1)} %copy.31), calls=%async_computation.1 | async-start | bytes 8192 | tf_op jit(solution)/shard_map/all_to_all | solution.py:45
  24.9 1.1 convolution_convert_fusion
  26.0 5.3 %all-to-all-done.1 = bf16[8,1,9]{2,1,0:T(2,128)(2,1)S(1)} async-done(((bf16[8,1,9]{2,1,0:T(2,128)(2,1)}), bf16[8,1,9]{2,1,0:T(2,128)(2,1)S(1)}, u32[]{:S(2)}, u32[]{:S(2)}) %all-to-all-start.1) | async-done | bytes 176 | tf_op jit(solution)/shard_map/all_to_all | solution.py:45
  31.3 3.5 all-to-all-start.2
  34.9 12.0 %all-to-all-done.2 = bf16[8,9,2048]{2,1,0:T(8,128)(2,1)S(1)} async-done(((bf16[8,9,2048]{2,1,0:T(8,128)(2,1)}), bf16[8,9,2048]{2,1,0:T(8,128)(2,1)S(1)}, u32[]{:S(2)}, u32[]{:S(2)}) %all-to-all-start.2) | async-done | bytes 294944 | tf_op jit(solution)/shard_map/all_to_all | solution.py:44
  47.1 15.5 %multiply_reduce_fusion = (f32[72]{0:T(128)S(1)}, bf16[1,72,7680]{2,1,0:T(8,128)(2,1)}) fusion(bf16[1,72,7680]{2,1,0:T(8,128)(2,1)S(1)} %copy-done.2, f32[72]{0:T(128)S(1)} %reshape.65, bf16[72,2048]{1,0:T(8,128)(2,1)S(1)} %reshape.63, bf16[7680,2048]{1,0:T(8,128)(2,1)} %param.9), kind=kOutput, calls=%fused_computation.4 | convolution fusion | flops 2267688960 | bytes 33964608 | tf_op jit(solution)/shard_map/dot_general | solution.py:51
  62.6 0.7 all_to_all.36
  63.3 3.7 %all-to-all-start.3 = ((f32[8,1,9]{2,1,0:T(1,128)}), f32[8,1,9]{2,1,0:T(1,128)S(1)}, u32[]{:S(2)}, u32[]{:S(2)}) async-start(f32[8,1,9]{2,1,0:T(1,128)} %bitcast.12), calls=%async_computation.3 | async-start | bytes 8192 | tf_op jit(solution)/shard_map/all_to_all | solution.py:58
  67.3 6.1 %all-to-all-done.3 = f32[8,1,9]{2,1,0:T(1,128)S(1)} async-done(((f32[8,1,9]{2,1,0:T(1,128)}), f32[8,1,9]{2,1,0:T(1,128)S(1)}, u32[]{:S(2)}, u32[]{:S(2)}) %all-to-all-start.3) | async-done | bytes 320 | tf_op jit(solution)/shard_map/all_to_all | solution.py:58
  73.6 0.8 convolution_bitcast_fusion
  74.5 13.9 %convert_bitcast_fusion = bf16[7680,2048]{0,1:T(8,128)(2,1)} fusion(bf16[72,2048]{1,0:T(8,128)(2,1)S(1)} %convert_element_type.93, bf16[1,72,7680]{2,1,0:T(8,128)(2,1)S(1)} %copy-done.2), kind=kOutput, calls=%fused_computation | convolution fusion | flops 2280652800 | bytes 32858112 | tf_op jit(solution)/shard_map/dot_general | solution.py:74
  88.4 40.7 %copy.43 = bf16[7680,2048]{1,0:T(8,128)(2,1)} copy(bf16[7680,2048]{0,1:T(8,128)(2,1)} %convert_bitcast_fusion) | data formatting | bytes 62914560
  129.1 0.7 copy-done.3
  129.8 1.0 convolution_convert_fusion.1
  130.8 159.6 %all-reduce.2.cloned.1.call-done = f32[2048,8]{0,1:T(8,128)} async-done(((f32[2048,8]{0,1:T(8,128)}), f32[2048,8]{0,1:T(8,128)}) %all-reduce.2.cloned.1.call-update) | async-done | bytes 65552 | tf_op jit(solution)/shard_map/psum | solution.py:72
  290.4 59.9 %reduce-scatter.4.cloned.1.call-done = bf16[1920,2048]{1,0:T(8,128)(2,1)} async-done(((bf16[7680,2048]{1,0:T(8,128)(2,1)}), bf16[1920,2048]{1,0:T(8,128)(2,1)}) %reduce-scatter.4.cloned.1.call-update) | async-done | bytes 7864336
  350.2 1.5 copy.55
  (37 shorter events, 1.9 us)
Async XLA Ops:
  8.0 16.9 %copy-start = (bf16[32,2048]{1,0:T(8,128)(2,1)S(1)}, bf16[32,2048]{1,0:T(8,128)(2,1)}, u32[]{:S(2)}) copy-start(bf16[32,2048]{1,0:T(8,128)(2,1)} %param.11) | copy-start | bytes 393220
  8.0 39.1 %copy-start.2 = (bf16[1,72,7680]{2,1,0:T(8,128)(2,1)S(1)}, bf16[1,72,7680]{2,1,0:T(8,128)(2,1)}, u32[]{:S(2)}) copy-start(bf16[1,72,7680]{2,1,0:T(8,128)(2,1)} %param.10) | copy-start | bytes 3317764
  8.0 8.9 %all-to-all-start = ((bf16[2,32,1024]{2,1,0:T(8,128)(2,1)}), bf16[2,32,1024]{2,1,0:T(8,128)(2,1)S(1)}, u32[]{:S(2)}, u32[]{:S(2)}) async-start(bf16[2,32,1024]{2,1,0:T(8,128)(2,1)} %bitcast.52), calls=%async_computation | async-start | bytes 262144 | tf_op jit(solution)/shard_map/all_to_all | solution.py:17
  19.5 11.8 %all-to-all-start.1 = ((bf16[8,1,9]{2,1,0:T(2,128)(2,1)}), bf16[8,1,9]{2,1,0:T(2,128)(2,1)S(1)}, u32[]{:S(2)}, u32[]{:S(2)}) async-start(bf16[8,1,9]{2,1,0:T(2,128)(2,1)} %copy.31), calls=%async_computation.1 | async-start | bytes 8192 | tf_op jit(solution)/shard_map/all_to_all | solution.py:45
  31.3 15.6 %all-to-all-start.2 = ((bf16[8,9,2048]{2,1,0:T(8,128)(2,1)}), bf16[8,9,2048]{2,1,0:T(8,128)(2,1)S(1)}, u32[]{:S(2)}, u32[]{:S(2)}) async-start(bf16[8,9,2048]{2,1,0:T(8,128)(2,1)} %convolution_convert_fusion), calls=%async_computation.2 | async-start | bytes 1048576 | tf_op jit(solution)/shard_map/all_to_all | solution.py:44
  47.1 26.5 %copy-start.4 = (s32[32,2]{0,1:T(2,128)S(1)}, s32[32,2]{0,1:T(2,128)}, u32[]{:S(2)}) copy-start(s32[32,2]{0,1:T(2,128)} %param.8) | copy-start | bytes 772
  63.3 10.1 %all-to-all-start.3 = ((f32[8,1,9]{2,1,0:T(1,128)}), f32[8,1,9]{2,1,0:T(1,128)S(1)}, u32[]{:S(2)}, u32[]{:S(2)}) async-start(f32[8,1,9]{2,1,0:T(1,128)} %bitcast.12), calls=%async_computation.3 | async-start | bytes 8192 | tf_op jit(solution)/shard_map/all_to_all | solution.py:58
  67.0 223.4 %all-reduce.2.cloned.1.call-start = ((), (), s32[]{:S(2)}) async-start(), calls=%async_computation.5 | async-start | bytes 131072 | tf_op jit(solution)/shard_map/psum | solution.py:72
  74.5 275.8 %reduce-scatter.4.cloned.1.call-start = ((), (), s32[]{:S(2)}) async-start(), calls=%async_computation.6 | async-start | bytes 39321600
  129.0 0.8 copy-start.3
  129.8 221.9 %copy-start.1 = (bf16[32,2048]{1,0:T(8,128)(2,1)S(1)}, bf16[32,2048]{1,0:T(8,128)(2,1)}, u32[]{:S(2)}) copy-start(bf16[32,2048]{1,0:T(8,128)(2,1)} %param.11) | copy-start | bytes 393220
Sparse Core Ops, SparseCore 0:
  74.6 215.7 all-reduce.1
Sparse Core Ops, SparseCore 1:
  129.2 221.0 reduce-scatter.3
where the time goes:
time: 361 us; the launch traced here: 359 us
  waiting for transfers between devices  245 us (68%)
  local copies, waits for them, and re-layouts  45.8 us (13%)
  matrix products  33.3 us (9%)
  starting transfers between devices  17 us (5%)
  between operations  15.6 us (4%)
    psum x1, waiting for transfers between devices, per_device(): router_grad = lax.psum(router_local, ('dp', 'expert', 'tensor'))  160 us
    unnamed x3, waiting for transfers between devices  59.9 us
    unnamed x14, local copies, waits for them, and re-layouts  43.7 us
    dot_general x1, matrix products, per_device(): lax.dot_general(recv_grad, down_weight, (((1,), (1,)), ((), ())), preferr...  15.5 us
    dot_general x1, matrix products, per_device(): lax.dot_general(hidden_rows, gated_grad, (((0,), (0,)), ((), ())), prefer...  13.9 us
    all_to_all x1, waiting for transfers between devices, per_device(): lax.all_to_all(send_grad, ('expert', 'tensor'), split_axis=0, concat_axis...  12 us
  transfers between devices with their start and end apart: 6, of which 6 were waited for; matrix products, arithmetic and copies ran while one was open for 16% of the time, Pallas kernels for 0%

commit v1 on v0

--- a/solution.py
+++ b/solution.py
@@ -1,7 +1,17 @@
+import functools
 import jax
 import jax.numpy as jnp
 from jax import lax
 from jax.sharding import PartitionSpec as P
+
+
+def _start_records(field_in, bus_axis, named_axis):
+    for dev_i in (bus_axis, named_axis):
+        field_in = lax.psum(field_in, axis_name=dev_i)
+    return field_in
+
+
+draw_squares = functools.partial(_start_records, bus_axis=("expert", "tensor"), named_axis="dp")
 
 
 def per_device(router_input, router_weight, expert_ids, down_weight, hidden, grad_output):
@@ -69,7 +79,7 @@
     router_local = jnp.dot(
         full_input.astype(jnp.float32).T, logit_grad, precision=lax.Precision.HIGHEST
     )
-    router_grad = lax.psum(router_local, ("dp", "expert", "tensor"))
+    router_grad = draw_squares(router_local)
     weight_sum = lax.psum_scatter(
         lax.dot_general(
             hidden_rows, gated_grad, (((0,), (0,)), ((), ())), preferred_element_type=jnp.float32

time: 361 us -> 428 us (1.19)
  waiting for transfers between devices: 245 us -> 308 us
  blocking collectives: 0 us -> 9.96 us
    unnamed x3 -> x4, waiting for transfers between devices: 59.9 us -> 222 us
    psum x1 -> x2, waiting for transfers between devices: 160 us -> 66.4 us  [_start_records(): field_in = lax.psum(field_in, axis_name=dev_i)]
    all_to_all x0 -> x1, blocking collectives: none -> 9.96 us  [per_device(): lax.all_to_all(gate_partial, ('expert', 'tensor'), split_axis=0, concat_a...]
    all_to_all x1 -> x0, waiting for transfers between devices: 6.07 us -> none  [per_device(): lax.all_to_all(gate_partial, ('expert', 'tensor'), split_axis=0, concat_a...]
  transfers between devices with their start and end apart: 6 -> 6, of which waited for: 6 -> 5; matrix products, arithmetic and copies ran while one was open for 16% -> 14% of each run, Pallas kernels for 0% -> 0%
where the time goes in v1:
time: 428 us; the launch traced here: 426 us
  waiting for transfers between devices  308 us (72%)
  local copies, waits for them, and re-layouts  45.2 us (11%)
  matrix products  33.2 us (8%)
  between operations  13.9 us (3%)
  starting transfers between devices  13.4 us (3%)
  blocking collectives  9.96 us (2%)
    unnamed x4, waiting for transfers between devices  222 us
    psum x2, waiting for transfers between devices, _start_records(): field_in = lax.psum(field_in, axis_name=dev_i)  66.4 us
    unnamed x14, local copies, waits for them, and re-layouts  43.8 us
    dot_general x1, matrix products, per_device(): lax.dot_general(recv_grad, down_weight, (((1,), (1,)), ((), ())), preferr...  15.5 us
    dot_general x1, matrix products, per_device(): lax.dot_general(hidden_rows, gated_grad, (((0,), (0,)), ((), ())), prefer...  13.8 us
    all_to_all x1, waiting for transfers between devices, per_device(): lax.all_to_all(send_grad, ('expert', 'tensor'), split_axis=0, concat_axis...  12 us
    all_to_all x1, blocking collectives, per_device(): lax.all_to_all(gate_partial, ('expert', 'tensor'), split_axis=0, concat_a...  9.96 us
  transfers between devices with their start and end apart: 6, of which 5 were waited for; matrix products, arithmetic and copies ran while one was open for 14% of the time, Pallas kernels for 0%

profile of v1, /device:TPU:0, one launch (start us, length us, event | category | flops | bytes accessed | tf_op | source)
XLA Modules:
  0.0 426.0 jit_solution(9705284663293806943)
XLA Ops:
  7.2 4.4 %all-to-all-start = ((bf16[2,32,1024]{2,1,0:T(8,128)(2,1)}), bf16[2,32,1024]{2,1,0:T(8,128)(2,1)S(1)}, u32[]{:S(2)}, u32[]{:S(2)}) async-start(bf16[2,32,1024]{2,1,0:T(8,128)(2,1)} %bitcast.52), calls=%async_computation | async-start | bytes 262144 | tf_op jit(solution)/shard_map/all_to_all | solution.py:27
  11.6 0.8 copy.28
  12.3 0.7 convert_convert_fusion
  13.3 0.2 select_reduce_fusion
  13.7 2.4 all-to-all-done
  16.1 0.9 fusion.15
  17.0 0.7 multiply_reduce_fusion.3
  17.8 0.2 fusion.2
  18.1 0.6 copy.31
  18.7 5.4 %all-to-all-start.1 = ((bf16[8,1,9]{2,1,0:T(2,128)(2,1)}), bf16[8,1,9]{2,1,0:T(2,128)(2,1)S(1)}, u32[]{:S(2)}, u32[]{:S(2)}) async-start(bf16[8,1,9]{2,1,0:T(2,128)(2,1)} %copy.31), calls=%async_computation.1 | async-start | bytes 8192 | tf_op jit(solution)/shard_map/all_to_all | solution.py:55
  24.1 1.1 convolution_convert_fusion
  25.2 5.3 %all-to-all-done.1 = bf16[8,1,9]{2,1,0:T(2,128)(2,1)S(1)} async-done(((bf16[8,1,9]{2,1,0:T(2,128)(2,1)}), bf16[8,1,9]{2,1,0:T(2,128)(2,1)S(1)}, u32[]{:S(2)}, u32[]{:S(2)}) %all-to-all-start.1) | async-done | bytes 176 | tf_op jit(solution)/shard_map/all_to_all | solution.py:55
  30.5 3.5 all-to-all-start.2
  34.1 12.0 %all-to-all-done.2 = bf16[8,9,2048]{2,1,0:T(8,128)(2,1)S(1)} async-done(((bf16[8,9,2048]{2,1,0:T(8,128)(2,1)}), bf16[8,9,2048]{2,1,0:T(8,128)(2,1)S(1)}, u32[]{:S(2)}, u32[]{:S(2)}) %all-to-all-start.2) | async-done | bytes 294944 | tf_op jit(solution)/shard_map/all_to_all | solution.py:54
  46.3 15.5 %multiply_reduce_fusion = (f32[72]{0:T(128)S(1)}, bf16[1,72,7680]{2,1,0:T(8,128)(2,1)}) fusion(bf16[1,72,7680]{2,1,0:T(8,128)(2,1)S(1)} %copy-done.2, f32[72]{0:T(128)S(1)} %reshape.65, bf16[72,2048]{1,0:T(8,128)(2,1)S(1)} %reshape.63, bf16[7680,2048]{1,0:T(8,128)(2,1)} %param.9), kind=kOutput, calls=%fused_computation.4 | convolution fusion | flops 2267688960 | bytes 33964608 | tf_op jit(solution)/shard_map/dot_general | solution.py:61
  61.9 10.0 %all_to_all.42 = f32[8,1,9]{2,1,0:T(1,128)S(1)} all-to-all(f32[8,1,9]{2,1,0:T(1,128)S(1)} %bitcast.54), channel_id=1, replica_groups=mesh['dp'=4,'expert'=4,'tensor'=2] {'expert','tensor'}, dimensions={0} | all-to-all | bytes 576 | tf_op jit(solution)/shard_map/all_to_all | solution.py:68
  72.1 0.8 convolution_bitcast_fusion
  73.2 66.4 %all-reduce.3.cloned.1.call-done = f32[2048,8]{0,1:T(8,128)} async-done(((f32[2048,8]{0,1:T(8,128)}), f32[2048,8]{0,1:T(8,128)}) %all-reduce.3.cloned.1.call-update) | async-done | bytes 65552 | tf_op jit(solution)/shard_map/psum | solution.py:10
  139.7 13.8 %convert_bitcast_fusion = bf16[7680,2048]{0,1:T(8,128)(2,1)} fusion(bf16[72,2048]{1,0:T(8,128)(2,1)S(1)} %convert_element_type.93, bf16[1,72,7680]{2,1,0:T(8,128)(2,1)S(1)} %copy-done.2), kind=kOutput, calls=%fused_computation | convolution fusion | flops 2280652800 | bytes 32858112 | tf_op jit(solution)/shard_map/dot_general | solution.py:84
  153.4 40.7 %copy.43 = bf16[7680,2048]{1,0:T(8,128)(2,1)} copy(bf16[7680,2048]{0,1:T(8,128)(2,1)} %convert_bitcast_fusion) | data formatting | bytes 62914560
  194.2 0.7 copy-done.3
  194.9 1.0 convolution_convert_fusion.1
  195.9 222.1 %reduce-scatter.4.cloned.1.call-done = bf16[1920,2048]{1,0:T(8,128)(2,1)} async-done(((bf16[7680,2048]{1,0:T(8,128)(2,1)}), bf16[1920,2048]{1,0:T(8,128)(2,1)}) %reduce-scatter.4.cloned.1.call-update) | async-done | bytes 7864336
  418.0 1.5 copy.56
  (39 shorter events, 1.6 us)
Async XLA Ops:
  7.2 16.9 %copy-start = (bf16[32,2048]{1,0:T(8,128)(2,1)S(1)}, bf16[32,2048]{1,0:T(8,128)(2,1)}, u32[]{:S(2)}) copy-start(bf16[32,2048]{1,0:T(8,128)(2,1)} %param.11) | copy-start | bytes 393220
  7.2 39.1 %copy-start.2 = (bf16[1,72,7680]{2,1,0:T(8,128)(2,1)S(1)}, bf16[1,72,7680]{2,1,0:T(8,128)(2,1)}, u32[]{:S(2)}) copy-start(bf16[1,72,7680]{2,1,0:T(8,128)(2,1)} %param.10) | copy-start | bytes 3317764
  7.2 8.9 %all-to-all-start = ((bf16[2,32,1024]{2,1,0:T(8,128)(2,1)}), bf16[2,32,1024]{2,1,0:T(8,128)(2,1)S(1)}, u32[]{:S(2)}, u32[]{:S(2)}) async-start(bf16[2,32,1024]{2,1,0:T(8,128)(2,1)} %bitcast.52), calls=%async_computation | async-start | bytes 262144 | tf_op jit(solution)/shard_map/all_to_all | solution.py:27
  18.7 11.8 %all-to-all-start.1 = ((bf16[8,1,9]{2,1,0:T(2,128)(2,1)}), bf16[8,1,9]{2,1,0:T(2,128)(2,1)S(1)}, u32[]{:S(2)}, u32[]{:S(2)}) async-start(bf16[8,1,9]{2,1,0:T(2,128)(2,1)} %copy.31), calls=%async_computation.1 | async-start | bytes 8192 | tf_op jit(solution)/shard_map/all_to_all | solution.py:55
  30.5 15.6 %all-to-all-start.2 = ((bf16[8,9,2048]{2,1,0:T(8,128)(2,1)}), bf16[8,9,2048]{2,1,0:T(8,128)(2,1)S(1)}, u32[]{:S(2)}, u32[]{:S(2)}) async-start(bf16[8,9,2048]{2,1,0:T(8,128)(2,1)} %convolution_convert_fusion), calls=%async_computation.2 | async-start | bytes 1048576 | tf_op jit(solution)/shard_map/all_to_all | solution.py:54
  34.0 105.6 %all-reduce.3.cloned.1.call-start = ((), (), s32[]{:S(2)}) async-start(), calls=%async_computation.5 | async-start | bytes 131072 | tf_op jit(solution)/shard_map/psum | solution.py:10
  46.3 25.8 %copy-start.4 = (s32[32,2]{0,1:T(2,128)S(1)}, s32[32,2]{0,1:T(2,128)}, u32[]{:S(2)}) copy-start(s32[32,2]{0,1:T(2,128)} %param.8) | copy-start | bytes 772
  72.9 123.0 %all-reduce.5.cloned.1.call-start = ((), (), s32[]{:S(2)}) async-start(), calls=%async_computation.6 | async-start | bytes 131072 | tf_op jit(solution)/shard_map/psum | solution.py:10
  139.6 278.3 %reduce-scatter.4.cloned.1.call-start = ((), (), s32[]{:S(2)}) async-start(), calls=%async_computation.7 | async-start | bytes 39321600
  194.2 0.8 copy-start.3
  194.9 224.5 %copy-start.1 = (bf16[32,2048]{1,0:T(8,128)(2,1)S(1)}, bf16[32,2048]{1,0:T(8,128)(2,1)}, u32[]{:S(2)}) copy-start(bf16[32,2048]{1,0:T(8,128)(2,1)} %param.11) | copy-start | bytes 393220
Sparse Core Ops, SparseCore 0:
  73.0 66.5 all-reduce.2
  141.9 31.4 all-reduce.4
  194.3 223.5 reduce-scatter.3
